TPU v7x, 32 devices: a whole 2x2x4 slice. The times are simulated.
32 devices in a mesh: rows: 8 (over z, y), grp: 4 (over x, core).
Axes of the slice: x: 2, y: 2, z: 4, core: 2. Of those that a mesh axis runs over, the one named last changes fastest.
Arguments:
- owner: int32 [1024, 24, 3], P('rows', 'grp'), may hold values from 0 to 7, as said below
- offset: int32 [1024, 24, 3], P('rows', 'grp'), may hold values from 0 to 511
- tables: float32 [12, 4096, 128], P('grp', 'rows'), may hold values from -6 to 6
- w_first: bfloat16 [3072, 1024], P('grp'), may hold values from -0.109375 to 0.109375
- b_first: float32 [1024], replicated, may hold values from -3 to 3
- w_out: float32 [1024], replicated, may hold values from -0.1875 to 0.1875
- labels: int32 [1024], P('rows'), may hold values 0 or 1
Outputs:
- table_grad: float32 [12, 4096, 128], P('grp', 'rows')
- losses: float32 [1024], P(('rows', 'grp'))
Inputs may be any that keep to these rules, and one draw needn't show every extreme that they name: Of the lookups of one device (its 128 samples and 6 features, all three hashes) at most 1032 name one owner, and in every draw some owner gets exactly 1032. Among the lookups of one device to one owner for one table, at most 114 distinct offsets occur, and that bound is reached in every draw.
All inputs are finite; a program needn't handle non-finite values. No bound on the sum of `labels` on one device may be relied on, other than what follows from the above.
Results may differ from a plain program's by a relative error of at most 0.005.
Values may be sent and summed in bfloat16 or wider, within the bound.
A program may use at most 64 MiB of HBM per device.

v0:
```python
import jax
import jax.numpy as jnp
from jax import lax
from jax.sharding import PartitionSpec as P


def head_loss(pre_act, w_out, targets):
    gate_sig = jax.nn.sigmoid(pre_act)
    logits = jnp.sum(pre_act * gate_sig * w_out, axis=1)
    losses = jax.nn.softplus(logits) - targets * logits
    grad_logit = jax.nn.sigmoid(logits) - targets
    grad_pre = (
        grad_logit[:, None] * w_out * (gate_sig * (1.0 + pre_act * (1.0 - gate_sig)))
    ).astype(jnp.bfloat16)
    return (losses, grad_pre)


def run_starts(sorted_values, values_index):
    is_first = jnp.concatenate([jnp.ones((1,), bool), sorted_values[1:] != sorted_values[:-1]])
    return lax.cummax(jnp.where(is_first, values_index, 0), axis=0)


def body(owner, offset, tables, w_first, b_first, w_out, labels):
    row_devices = lax.axis_size("rows")
    bdev_rows, fgrp_count = (owner.shape[0], owner.shape[1])
    rows_dev, emb_width = (tables.shape[1], tables.shape[2])
    lookups = bdev_rows * fgrp_count * 3
    hot_count = 8 * (bdev_rows * fgrp_count * 7 // (16 * row_devices)) + 8
    owner_flat = owner.reshape(-1)
    offset_flat = offset.reshape(-1)
    positions = jnp.arange(lookups, dtype=jnp.int32)
    table_kind = positions % 3
    flat_table = tables.reshape(3 * rows_dev, emb_width)
    unique_cap = hot_count // 3
    group_key = (owner_flat * 3 + table_kind) * rows_dev + offset_flat
    ordering = jnp.argsort(group_key, stable=True)
    sorted_keys = group_key[ordering]
    is_new = jnp.concatenate([jnp.ones((1,), bool), sorted_keys[1:] != sorted_keys[:-1]])
    unique_id = jnp.cumsum(is_new.astype(jnp.int32)) - 1
    sorted_group = sorted_keys // rows_dev
    slot_sorted = sorted_group * unique_cap + unique_id - run_starts(sorted_group, unique_id)
    slot_of = jnp.zeros((lookups,), jnp.int32).at[ordering].set(slot_sorted)
    outgoing = jnp.full((row_devices * 3 * unique_cap,), -1, jnp.int32).at[slot_of].set(offset_flat)
    row_codes = lax.all_to_all(
        outgoing.reshape(row_devices, 3, unique_cap),
        "rows",
        split_axis=0,
        concat_axis=0,
        tiled=True,
    )
    is_live = (row_codes >= 0)[..., None]
    row_index = jnp.arange(3, dtype=jnp.int32)[None, :, None] * rows_dev + jnp.maximum(row_codes, 0)
    fetched = jnp.take(flat_table, row_index.reshape(-1), axis=0)
    fetched = (fetched.reshape(row_codes.shape + (emb_width,)) * is_live).astype(jnp.bfloat16)
    returned = lax.all_to_all(fetched, "rows", split_axis=0, concat_axis=0, tiled=True)
    owner_codes, returned = (row_codes, returned)
    owner_index = (
        jnp.arange(3, dtype=jnp.int32)[None, :, None] * rows_dev + jnp.maximum(owner_codes, 0)
    ).reshape(-1)
    looked = (
        returned.reshape(-1, emb_width)[slot_of]
        .astype(jnp.float32)
        .reshape(bdev_rows, fgrp_count, 3, emb_width)
    )
    embedded = looked[:, :, 0] * looked[:, :, 1] + looked[:, :, 2]
    features = embedded.reshape(bdev_rows, fgrp_count * emb_width).astype(jnp.bfloat16)
    targets = labels.astype(jnp.float32)
    share_rows = bdev_rows // lax.axis_size("grp")
    share_start = lax.axis_index("grp") * share_rows
    partial_pre = jnp.dot(features, w_first, preferred_element_type=jnp.float32)
    pre_act = lax.psum(partial_pre, "grp") + b_first
    all_losses, grad_pre = head_loss(pre_act, w_out, targets)
    losses = lax.dynamic_slice_in_dim(all_losses, share_start, share_rows, 0)
    grad_emb = jnp.dot(grad_pre, w_first.T, preferred_element_type=jnp.float32).reshape(
        bdev_rows, fgrp_count, emb_width
    )
    row_grads = jnp.stack(
        [grad_emb * looked[:, :, 1], grad_emb * looked[:, :, 0], grad_emb], axis=2
    ).reshape(lookups, emb_width)
    outgoing_grads = (
        jnp.zeros((row_devices * 3 * unique_cap, emb_width), jnp.float32).at[slot_of].add(row_grads)
    )
    received = lax.all_to_all(
        outgoing_grads.reshape(row_devices, 3, unique_cap, emb_width),
        "rows",
        split_axis=0,
        concat_axis=0,
        tiled=True,
    )
    table_grad = (
        jnp.zeros((3 * rows_dev, emb_width), jnp.float32)
        .at[owner_index]
        .add(received.reshape(-1, emb_width))
    )
    return (table_grad.reshape(3, rows_dev, emb_width), losses)


def solution(mesh):
    placed = (
        P("rows", "grp", None),
        P("rows", "grp", None),
        P("grp", "rows", None),
        P("grp", None),
        P(),
        P(),
        P("rows"),
    )
    return jax.shard_map(
        body,
        mesh=mesh,
        in_specs=placed,
        out_specs=(P("grp", "rows", None), P(("rows", "grp"))),
        check_vma=False,
    )
```

profile of v0, /device:TPU:0, one launch (start us, length us, event | category | flops | bytes accessed | tf_op | source)
XLA Modules:
  0.0 225.6 jit_solution(1120389095388177979)
XLA Ops:
  9.7 5.8 %sort.17 = (s32[2304]{0:T(1024)}, s32[2304]{0:T(1024)S(1)}) sort(s32[2304]{0:T(1024)S(1)} %fusion.12, s32[2304]{0:T(1024)S(1)} %iota.15), dimensions={0}, to_apply=%region_0.1 | sort | flops 27648 | bytes 36864 | tf_op jit(solution)/shard_map/jit(argsort)/sort | solution.py:36
  15.5 12.3 %gather_fusion = s32[2304]{0:T(1024)S(1)} fusion(s32[2304]{0:T(1024)S(1)} %fusion.12, s32[3072]{0:T(1024)S(1)} %pad_clamp_fusion.2), kind=kCustom, calls=%fused_computation | custom fusion | bytes 27648 | tf_op jit(solution)/shard_map/gather | solution.py:37
  29.2 9.0 %scatter_custom_fusion = s32[2304]{0:T(1024)S(1)} fusion(s32[2304]{0:T(1024)S(1)} %compare_select_fusion.3, s32[2304]{0:T(1024)S(1)} %bitcast_subtract_fusion, s32[]{:T(128)} %constant.33.clone.1), kind=kCustom, calls=%fused_computation.64 | custom fusion | bytes 9220 | tf_op jit(solution)/shard_map/scatter | solution.py:42
  38.2 9.0 %scatter_custom_fusion.1 = s32[2736]{0:T(1024)S(1)} fusion(s32[2304]{0:T(1024)S(1)} %compare_select_fusion.2, s32[2304]{0:T(1024)S(1)} %reshape.183, s32[]{:T(128)} %constant.31.clone.1), kind=kCustom, calls=%fused_computation.66 | custom fusion | bytes 10948 | tf_op jit(solution)/shard_map/scatter | solution.py:43
  48.0 7.3 %all-to-all-start = ((s32[8,3,114]{2,1,0:T(4,128)}), s32[8,3,114]{2,1,0:T(4,128)S(1)}, u32[]{:S(2)}, u32[]{:S(2)}) async-start(s32[8,3,114]{2,1,0:T(4,128)} %reshape.136), calls=%async_computation | async-start | bytes 32768 | tf_op jit(solution)/shard_map/all_to_all | solution.py:44
  55.3 6.6 %all-to-all-done = s32[8,3,114]{2,1,0:T(4,128)S(1)} async-done(((s32[8,3,114]{2,1,0:T(4,128)}), s32[8,3,114]{2,1,0:T(4,128)S(1)}, u32[]{:S(2)}, u32[]{:S(2)}) %all-to-all-start) | async-done | bytes 10976 | tf_op jit(solution)/shard_map/all_to_all | solution.py:44
  62.1 5.9 %gather_fusion.1 = f32[2736,128]{1,0:T(8,128)} fusion(f32[1536,128]{1,0:T(8,128)S(1)} %bitcast.21, s32[3072]{0:T(1024)S(1)} %pad_clamp_fusion.1), kind=kCustom, calls=%fused_computation.1 | custom fusion | bytes 2812608 | tf_op jit(solution)/shard_map/jit(_take)/gather | solution.py:53
  68.0 1.4 gather.14
  69.5 2.1 multiply_convert_fusion
  71.5 3.5 %all-to-all-start.1 = ((bf16[8,3,114,128]{3,2,1,0:T(8,128)(2,1)}), bf16[8,3,114,128]{3,2,1,0:T(8,128)(2,1)S(1)}, u32[]{:S(2)}, u32[]{:S(2)}) async-start(bf16[8,3,114,128]{3,2,1,0:T(8,128)(2,1)} %multiply_convert_fusion), calls=%async_computation.1 | async-start | bytes 1474560 | tf_op jit(solution)/shard_map/all_to_all | solution.py:55
  75.3 17.6 %all-to-all-done.1 = bf16[8,3,114,128]{3,2,1,0:T(8,128)(2,1)S(1)} async-done(((bf16[8,3,114,128]{3,2,1,0:T(8,128)(2,1)}), bf16[8,3,114,128]{3,2,1,0:T(8,128)(2,1)S(1)}, u32[]{:S(2)}, u32[]{:S(2)}) %all-to-all-start.1) | async-done | bytes 700448 | tf_op jit(solution)/shard_map/all_to_all | solution.py:55
  93.2 5.6 %gather_fusion.2 = bf16[2304,128]{1,0:T(8,128)(2,1)} fusion(bf16[2736,128]{1,0:T(8,128)(2,1)S(1)} %reshape.139, s32[3072]{0:T(1024)S(1)} %pad_clamp_fusion), kind=kCustom, calls=%fused_computation.2 | custom fusion | bytes 1188864 | tf_op jit(solution)/shard_map/gather | solution.py:61
  98.8 2.0 reshape.146
  102.7 1.2 fusion.28
  103.9 32.6 %all-reduce.2.cloned.1.call-done = f32[128,1024]{1,0:T(8,128)} async-done(((f32[128,1024]{1,0:T(8,128)}), f32[128,1024]{1,0:T(8,128)}) %all-reduce.2.cloned.1.call-update) | async-done | bytes 524304 | tf_op jit(solution)/shard_map/psum | solution.py:71
  136.5 1.3 multiply_reduce_fusion
  137.8 1.8 fusion.5
  140.8 1.4 reshape.191
  142.1 14.9 %scatter_custom_fusion.2 = f32[2736,128]{1,0:T(8,128)S(1)} fusion(s32[2304]{0:T(1024)} %copy-done.4, f32[2304,128]{1,0:T(8,128)} %reshape.191, f32[]{:T(128)} %constant.26.clone.1), kind=kCustom, calls=%fused_computation.9 | custom fusion | flops 294912 | bytes 1401344 | tf_op jit(solution)/shard_map/scatter-add | solution.py:81
  157.1 1.2 reshape.142
  158.3 5.5 %all-to-all-start.2 = ((f32[8,3,114,128]{3,2,1,0:T(8,128)}), f32[8,3,114,128]{3,2,1,0:T(8,128)S(1)}, u32[]{:S(2)}, u32[]{:S(2)}) async-start(f32[8,3,114,128]{3,2,1,0:T(8,128)} %reshape.142), calls=%async_computation.2 | async-start | bytes 2949120 | tf_op jit(solution)/shard_map/all_to_all | solution.py:83
  164.4 33.5 %all-to-all-done.2 = f32[8,3,114,128]{3,2,1,0:T(8,128)S(1)} async-done(((f32[8,3,114,128]{3,2,1,0:T(8,128)}), f32[8,3,114,128]{3,2,1,0:T(8,128)S(1)}, u32[]{:S(2)}, u32[]{:S(2)}) %all-to-all-start.2) | async-done | bytes 1400864 | tf_op jit(solution)/shard_map/all_to_all | solution.py:83
  197.9 1.2 reshape.199
  199.1 19.7 %scatter_custom_fusion.3 = f32[1536,128]{1,0:T(8,128)} fusion(s32[2736]{0:T(1024)S(1)} %fusion.20, f32[2736,128]{1,0:T(8,128)} %reshape.199, f32[]{:T(128)} %constant.26.clone.1), kind=kCustom, calls=%fused_computation.16 | custom fusion | flops 350208 | bytes 786944 | tf_op jit(solution)/shard_map/scatter-add | solution.py:93
  (59 shorter events, 8.9 us)
Async XLA Ops:
  7.2 95.5 %copy-start = (bf16[768,1024]{1,0:T(8,128)(2,1)S(1)}, bf16[768,1024]{1,0:T(8,128)(2,1)}, u32[]{:S(2)}) copy-start(bf16[768,1024]{1,0:T(8,128)(2,1)} %param.10) | copy-start | bytes 4718596
  15.4 46.7 %copy-start.1 = (f32[3,512,128]{2,1,0:T(8,128)S(1)}, f32[3,512,128]{2,1,0:T(8,128)}, u32[]{:S(2)}) copy-start(f32[3,512,128]{2,1,0:T(8,128)} %param.9) | copy-start | bytes 2359300
  38.2 37.1 %copy-start.4 = (s32[2304]{0:T(1024)}, s32[2304]{0:T(1024)S(1)}, u32[]{:S(2)}) copy-start(s32[2304]{0:T(1024)S(1)} %compare_select_fusion.2) | copy-start | bytes 27652
  48.0 13.9 %all-to-all-start = ((s32[8,3,114]{2,1,0:T(4,128)}), s32[8,3,114]{2,1,0:T(4,128)S(1)}, u32[]{:S(2)}, u32[]{:S(2)}) async-start(s32[8,3,114]{2,1,0:T(4,128)} %reshape.136), calls=%async_computation | async-start | bytes 32768 | tf_op jit(solution)/shard_map/all_to_all | solution.py:44
  71.5 21.4 %all-to-all-start.1 = ((bf16[8,3,114,128]{3,2,1,0:T(8,128)(2,1)}), bf16[8,3,114,128]{3,2,1,0:T(8,128)(2,1)S(1)}, u32[]{:S(2)}, u32[]{:S(2)}) async-start(bf16[8,3,114,128]{3,2,1,0:T(8,128)(2,1)} %multiply_convert_fusion), calls=%async_computation.1 | async-start | bytes 1474560 | tf_op jit(solution)/shard_map/all_to_all | solution.py:55
  75.1 61.4 %all-reduce.2.cloned.1.call-start = ((), (), s32[]{:S(2)}) async-start(), calls=%async_computation.3 | async-start | bytes 1048576 | tf_op jit(solution)/shard_map/psum | solution.py:71
  101.6 0.8 copy-start.2
  102.6 33.8 %copy-start.5 = (f32[1024]{0:T(1024)S(1)}, f32[1024]{0:T(1024)}, u32[]{:S(2)}) copy-start(f32[1024]{0:T(1024)} %param.12) | copy-start | bytes 12292
  102.6 33.8 %copy-start.6 = (f32[1024]{0:T(1024)S(1)}, f32[1024]{0:T(1024)}, u32[]{:S(2)}) copy-start(f32[1024]{0:T(1024)} %param.11) | copy-start | bytes 12292
  102.7 35.1 %copy-start.7 = (s32[128]{0:T(128)S(1)}, s32[128]{0:T(128)}, u32[]{:S(2)}) copy-start(s32[128]{0:T(128)} %param.13) | copy-start | bytes 1540
  137.8 2.0 copy-start.3
  158.3 39.6 %all-to-all-start.2 = ((f32[8,3,114,128]{3,2,1,0:T(8,128)}), f32[8,3,114,128]{3,2,1,0:T(8,128)S(1)}, u32[]{:S(2)}, u32[]{:S(2)}) async-start(f32[8,3,114,128]{3,2,1,0:T(8,128)} %reshape.142), calls=%async_computation.2 | async-start | bytes 2949120 | tf_op jit(solution)/shard_map/all_to_all | solution.py:83
Sparse Core Ops, SparseCore 0:
  104.0 32.4 all-reduce.1
where the time goes:
time: 226 us
  waiting for transfers between devices  90.3 us (40%)
  local copies, waits for them, and re-layouts  55.4 us (25%)
  other arithmetic  46 us (20%)
  starting transfers between devices  16.6 us (7%)
  between operations  14.3 us (6%)
  matrix products  3 us (1%)
    all_to_all x1, waiting for transfers between devices, body(): lax.all_to_all(outgoing_grads.reshape(row_devices, 3, unique_cap, emb_wid...  33.5 us
    psum x1, waiting for transfers between devices, body(): pre_act = lax.psum(partial_pre, 'grp') + b_first  32.6 us
    scatter-add x1, other arithmetic, body(): table_grad = jnp.zeros((3 * rows_dev, emb_width), jnp.float32).at[owner_i...  19.7 us
    all_to_all x1, waiting for transfers between devices, body(): lax.all_to_all(fetched, 'rows', split_axis=0, concat_axis=0, tiled=True)  17.6 us
    scatter-add x1, other arithmetic, body(): jnp.zeros((row_devices * 3 * unique_cap, emb_width), jnp.float32)  14.9 us
    gather x1, local copies, waits for them, and re-layouts, body(): sorted_keys = group_key[ordering]  12.3 us
    scatter x1, local copies, waits for them, and re-layouts, body(): slot_of = jnp.zeros((lookups,), jnp.int32).at[ordering].set(slot_sorted)  9 us
    scatter x1, local copies, waits for them, and re-layouts, body(): jnp.full((row_devices * 3 * unique_cap,), -1, jnp.int32).at[slot_of]  8.99 us
  transfers between devices with their start and end apart: 4, of which 4 were waited for; matrix products, arithmetic and copies ran while one was open for 0% of the time, Pallas kernels for 0%

commit v1 on v0

--- a/solution.py
+++ b/solution.py
@@ -68,7 +68,7 @@
     share_rows = bdev_rows // lax.axis_size("grp")
     share_start = lax.axis_index("grp") * share_rows
     partial_pre = jnp.dot(features, w_first, preferred_element_type=jnp.float32)
-    pre_act = lax.psum(partial_pre, "grp") + b_first
+    pre_act = jnp.sum(lax.all_gather(partial_pre, "grp"), axis=0) + b_first
     all_losses, grad_pre = head_loss(pre_act, w_out, targets)
     losses = lax.dynamic_slice_in_dim(all_losses, share_start, share_rows, 0)
     grad_emb = jnp.dot(grad_pre, w_first.T, preferred_element_type=jnp.float32).reshape(

time: 226 us -> 218 us (0.965)
  waiting for transfers between devices: 90.3 us -> 80.6 us
    psum x1 -> x0, waiting for transfers between devices: 32.6 us -> none  [body(): pre_act = lax.psum(partial_pre, 'grp') + b_first]
    all_gather x0 -> x1, waiting for transfers between devices: none -> 21.7 us  [body(): pre_act = jnp.sum(lax.all_gather(partial_pre, 'grp'), axis=0) + b_first]
where the time goes in v1:
time: 218 us; the launch traced here: 217 us
  waiting for transfers between devices  80.6 us (37%)
  local copies, waits for them, and re-layouts  56.5 us (26%)
  other arithmetic  46.6 us (21%)
  starting transfers between devices  16.6 us (8%)
  between operations  14.3 us (7%)
  matrix products  2.66 us (1%)
    all_to_all x1, waiting for transfers between devices, body(): lax.all_to_all(outgoing_grads.reshape(row_devices, 3, unique_cap, emb_wid...  34.7 us
    all_gather x1, waiting for transfers between devices, body(): pre_act = jnp.sum(lax.all_gather(partial_pre, 'grp'), axis=0) + b_first  21.7 us
    scatter-add x1, other arithmetic, body(): table_grad = jnp.zeros((3 * rows_dev, emb_width), jnp.float32).at[owner_i...  19.7 us
    all_to_all x1, waiting for transfers between devices, body(): lax.all_to_all(fetched, 'rows', split_axis=0, concat_axis=0, tiled=True)  17.6 us
    scatter-add x1, other arithmetic, body(): jnp.zeros((row_devices * 3 * unique_cap, emb_width), jnp.float32)  14.9 us
    gather x1, local copies, waits for them, and re-layouts, body(): sorted_keys = group_key[ordering]  12.3 us
    scatter x1, local copies, waits for them, and re-layouts, body(): slot_of = jnp.zeros((lookups,), jnp.int32).at[ordering].set(slot_sorted)  9 us
    scatter x1, local copies, waits for them, and re-layouts, body(): jnp.full((row_devices * 3 * unique_cap,), -1, jnp.int32).at[slot_of]  8.99 us
  transfers between devices with their start and end apart: 4, of which 4 were waited for; matrix products, arithmetic and copies ran while one was open for 0% of the time, Pallas kernels for 0%

profile of v1, /device:TPU:0, one launch (start us, length us, event | category | flops | bytes accessed | tf_op | source)
XLA Modules:
  0.0 217.4 jit_solution(17948422743095148726)
XLA Ops:
  9.7 5.8 %sort.17 = (s32[2304]{0:T(1024)}, s32[2304]{0:T(1024)S(1)}) sort(s32[2304]{0:T(1024)S(1)} %fusion.12, s32[2304]{0:T(1024)S(1)} %iota.15), dimensions={0}, to_apply=%region_0.1 | sort | flops 27648 | bytes 36864 | tf_op jit(solution)/shard_map/jit(argsort)/sort | solution.py:36
  15.5 12.3 %gather_fusion = s32[2304]{0:T(1024)S(1)} fusion(s32[2304]{0:T(1024)S(1)} %fusion.12, s32[3072]{0:T(1024)S(1)} %pad_clamp_fusion.2), kind=kCustom, calls=%fused_computation | custom fusion | bytes 27648 | tf_op jit(solution)/shard_map/gather | solution.py:37
  29.2 9.0 %scatter_custom_fusion = s32[2304]{0:T(1024)S(1)} fusion(s32[2304]{0:T(1024)S(1)} %compare_select_fusion.3, s32[2304]{0:T(1024)S(1)} %bitcast_subtract_fusion, s32[]{:T(128)} %constant.33.clone.1), kind=kCustom, calls=%fused_computation.64 | custom fusion | bytes 9220 | tf_op jit(solution)/shard_map/scatter | solution.py:42
  38.2 9.0 %scatter_custom_fusion.1 = s32[2736]{0:T(1024)S(1)} fusion(s32[2304]{0:T(1024)S(1)} %compare_select_fusion.2, s32[2304]{0:T(1024)S(1)} %reshape.183, s32[]{:T(128)} %constant.31.clone.1), kind=kCustom, calls=%fused_computation.66 | custom fusion | bytes 10948 | tf_op jit(solution)/shard_map/scatter | solution.py:43
  48.0 7.3 %all-to-all-start = ((s32[8,3,114]{2,1,0:T(4,128)}), s32[8,3,114]{2,1,0:T(4,128)S(1)}, u32[]{:S(2)}, u32[]{:S(2)}) async-start(s32[8,3,114]{2,1,0:T(4,128)} %reshape.136), calls=%async_computation | async-start | bytes 32768 | tf_op jit(solution)/shard_map/all_to_all | solution.py:44
  55.3 6.6 %all-to-all-done = s32[8,3,114]{2,1,0:T(4,128)S(1)} async-done(((s32[8,3,114]{2,1,0:T(4,128)}), s32[8,3,114]{2,1,0:T(4,128)S(1)}, u32[]{:S(2)}, u32[]{:S(2)}) %all-to-all-start) | async-done | bytes 10976 | tf_op jit(solution)/shard_map/all_to_all | solution.py:44
  62.1 5.9 %gather_fusion.1 = f32[2736,128]{1,0:T(8,128)} fusion(f32[1536,128]{1,0:T(8,128)S(1)} %bitcast.20, s32[3072]{0:T(1024)S(1)} %pad_clamp_fusion.1), kind=kCustom, calls=%fused_computation.1 | custom fusion | bytes 2812608 | tf_op jit(solution)/shard_map/jit(_take)/gather | solution.py:53
  68.0 1.4 gather.14
  69.5 2.1 multiply_convert_fusion
  71.5 3.5 %all-to-all-start.1 = ((bf16[8,3,114,128]{3,2,1,0:T(8,128)(2,1)}), bf16[8,3,114,128]{3,2,1,0:T(8,128)(2,1)S(1)}, u32[]{:S(2)}, u32[]{:S(2)}) async-start(bf16[8,3,114,128]{3,2,1,0:T(8,128)(2,1)} %multiply_convert_fusion), calls=%async_computation.1 | async-start | bytes 1474560 | tf_op jit(solution)/shard_map/all_to_all | solution.py:55
  75.3 17.6 %all-to-all-done.1 = bf16[8,3,114,128]{3,2,1,0:T(8,128)(2,1)S(1)} async-done(((bf16[8,3,114,128]{3,2,1,0:T(8,128)(2,1)}), bf16[8,3,114,128]{3,2,1,0:T(8,128)(2,1)S(1)}, u32[]{:S(2)}, u32[]{:S(2)}) %all-to-all-start.1) | async-done | bytes 700448 | tf_op jit(solution)/shard_map/all_to_all | solution.py:55
  93.2 5.6 %gather_fusion.2 = bf16[2304,128]{1,0:T(8,128)(2,1)} fusion(bf16[2736,128]{1,0:T(8,128)(2,1)S(1)} %reshape.139, s32[3072]{0:T(1024)S(1)} %pad_clamp_fusion), kind=kCustom, calls=%fused_computation.2 | custom fusion | bytes 1188864 | tf_op jit(solution)/shard_map/gather | solution.py:61
  98.8 2.0 reshape.146
  102.6 1.2 fusion.28
  103.9 21.7 %all-gather.3.cloned.1.call-done = f32[512,1024]{1,0:T(8,128)} async-done(((f32[128,1024]{1,0:T(8,128)}), f32[512,1024]{1,0:T(8,128)}) %all-gather.3.cloned.1.call-update) | async-done | bytes 2097168 | tf_op jit(solution)/shard_map/all_gather | solution.py:71
  125.6 1.8 reduce_sum.18
  127.7 1.5 fusion.5
  131.3 1.4 reshape.191
  132.7 14.9 %scatter_custom_fusion.2 = f32[2736,128]{1,0:T(8,128)S(1)} fusion(s32[2304]{0:T(1024)} %copy-done.4, f32[2304,128]{1,0:T(8,128)} %reshape.191, f32[]{:T(128)} %constant.26.clone.1), kind=kCustom, calls=%fused_computation.9 | custom fusion | flops 294912 | bytes 1401344 | tf_op jit(solution)/shard_map/scatter-add | solution.py:81
  147.6 1.2 reshape.142
  148.8 5.5 %all-to-all-start.2 = ((f32[8,3,114,128]{3,2,1,0:T(8,128)}), f32[8,3,114,128]{3,2,1,0:T(8,128)S(1)}, u32[]{:S(2)}, u32[]{:S(2)}) async-start(f32[8,3,114,128]{3,2,1,0:T(8,128)} %reshape.142), calls=%async_computation.2 | async-start | bytes 2949120 | tf_op jit(solution)/shard_map/all_to_all | solution.py:83
  154.9 34.7 %all-to-all-done.2 = f32[8,3,114,128]{3,2,1,0:T(8,128)S(1)} async-done(((f32[8,3,114,128]{3,2,1,0:T(8,128)}), f32[8,3,114,128]{3,2,1,0:T(8,128)S(1)}, u32[]{:S(2)}, u32[]{:S(2)}) %all-to-all-start.2) | async-done | bytes 1400864 | tf_op jit(solution)/shard_map/all_to_all | solution.py:83
  189.6 1.2 reshape.199
  190.8 19.7 %scatter_custom_fusion.3 = f32[1536,128]{1,0:T(8,128)} fusion(s32[2736]{0:T(1024)S(1)} %fusion.20, f32[2736,128]{1,0:T(8,128)} %reshape.199, f32[]{:T(128)} %constant.26.clone.1), kind=kCustom, calls=%fused_computation.16 | custom fusion | flops 350208 | bytes 786944 | tf_op jit(solution)/shard_map/scatter-add | solution.py:93
  (60 shorter events, 10.1 us)
Async XLA Ops:
  7.2 95.5 %copy-start = (bf16[768,1024]{1,0:T(8,128)(2,1)S(1)}, bf16[768,1024]{1,0:T(8,128)(2,1)}, u32[]{:S(2)}) copy-start(bf16[768,1024]{1,0:T(8,128)(2,1)} %param.10) | copy-start | bytes 4718596
  15.4 46.7 %copy-start.1 = (f32[3,512,128]{2,1,0:T(8,128)S(1)}, f32[3,512,128]{2,1,0:T(8,128)}, u32[]{:S(2)}) copy-start(f32[3,512,128]{2,1,0:T(8,128)} %param.9) | copy-start | bytes 2359300
  38.2 37.1 %copy-start.4 = (s32[2304]{0:T(1024)}, s32[2304]{0:T(1024)S(1)}, u32[]{:S(2)}) copy-start(s32[2304]{0:T(1024)S(1)} %compare_select_fusion.2) | copy-start | bytes 27652
  48.0 13.9 %all-to-all-start = ((s32[8,3,114]{2,1,0:T(4,128)}), s32[8,3,114]{2,1,0:T(4,128)S(1)}, u32[]{:S(2)}, u32[]{:S(2)}) async-start(s32[8,3,114]{2,1,0:T(4,128)} %reshape.136), calls=%async_computation | async-start | bytes 32768 | tf_op jit(solution)/shard_map/all_to_all | solution.py:44
  71.5 21.4 %all-to-all-start.1 = ((bf16[8,3,114,128]{3,2,1,0:T(8,128)(2,1)}), bf16[8,3,114,128]{3,2,1,0:T(8,128)(2,1)S(1)}, u32[]{:S(2)}, u32[]{:S(2)}) async-start(bf16[8,3,114,128]{3,2,1,0:T(8,128)(2,1)} %multiply_convert_fusion), calls=%async_computation.1 | async-start | bytes 1474560 | tf_op jit(solution)/shard_map/all_to_all | solution.py:55
  75.1 50.5 %all-gather.3.cloned.1.call-start = ((), (), s32[]{:S(2)}) async-start(), calls=%async_computation.3 | async-start | bytes 2621440 | tf_op jit(solution)/shard_map/all_gather | solution.py:71
  101.6 0.8 copy-start.2
  103.9 23.5 %copy-start.5 = (f32[1024]{0:T(1024)S(1)}, f32[1024]{0:T(1024)}, u32[]{:S(2)}) copy-start(f32[1024]{0:T(1024)} %param.12) | copy-start | bytes 12292
  103.9 23.5 %copy-start.6 = (f32[1024]{0:T(1024)S(1)}, f32[1024]{0:T(1024)}, u32[]{:S(2)}) copy-start(f32[1024]{0:T(1024)} %param.11) | copy-start | bytes 12292
  125.6 2.1 copy-start.7
  127.7 2.6 %copy-start.3 = (f32[128,6,1,128]{3,2,1,0:T(1,128)S(1)}, f32[128,6,1,128]{3,2,1,0:T(1,128)}, u32[]{:S(2)}) copy-start(f32[128,6,1,128]{3,2,1,0:T(1,128)} %copy-done.2) | copy-start | bytes 1179652
  148.8 40.8 %all-to-all-start.2 = ((f32[8,3,114,128]{3,2,1,0:T(8,128)}), f32[8,3,114,128]{3,2,1,0:T(8,128)S(1)}, u32[]{:S(2)}, u32[]{:S(2)}) async-start(f32[8,3,114,128]{3,2,1,0:T(8,128)} %reshape.142), calls=%async_computation.2 | async-start | bytes 2949120 | tf_op jit(solution)/shard_map/all_to_all | solution.py:83
Sparse Core Ops, SparseCore 0:
  104.0 21.5 all-gather.2
